TPU v7x, 32 devices: a whole 2x2x4 slice. The times are simulated.
32 devices in a mesh: row: 8 (over z, x), col: 4 (over y, core).
Axes of the slice: x: 2, y: 2, z: 4, core: 2. Of those that a mesh axis runs over, the one named last changes fastest.
Arguments:
- sparse_blocks: float32 [4096, 128, 128], P(('row', 'col')), may hold values from -0.5 to 0.5
- panel_rows: float32 [262144, 128], P(('row', 'col')), may hold values from -6 to 6
- block_row: int32 [4096], P(('row', 'col')), may hold values from 0 to 63
- block_owner: int32 [4096, 1], P(('row', 'col')), may hold values from 0 to 31; in each aligned block of 128 rows (0 to 127, 128 to 255, ...) at most 8 rows name the same one
- block_offset: int32 [4096], P(('row', 'col')), may hold values from 0 to 63
Outputs:
- result: float32 [262144, 128], P(('row', 'col'))
Inputs may be any that keep to these rules, and one draw needn't show every extreme that they name: `block_owner`: among the blocks of one device, at most 8 name the same owner, a bound that some block reaches.
All inputs are finite; a program needn't handle non-finite values.
Results may differ from a plain program's by a relative error of at most 0.0001.
Values sent between devices are 32-bit elements; how exact they have to be, the bound alone decides.
A program may use at most 192 MiB of HBM per device.

v0:
```python
import jax
import jax.numpy as jnp
from jax import lax
from jax.sharding import PartitionSpec as P


def merge_lead(array):
    return array.reshape((array.shape[0] * array.shape[1],) + array.shape[2:])


def relay_single(send_products, labels):
    return (
        lax.all_to_all(
            merge_lead(send_products), ("row", "col"), split_axis=0, concat_axis=0, tiled=True
        ),
        lax.all_to_all(merge_lead(labels), ("row", "col"), split_axis=0, concat_axis=0, tiled=True),
    )


def body(sparse_blocks, panel_rows, block_row, block_owner, block_offset):
    row_count = lax.axis_size("row")
    col_count = lax.axis_size("col")
    device_count = row_count * col_count
    slot_count = sparse_blocks.shape[0]
    block_size = sparse_blocks.shape[1]
    width = panel_rows.shape[1]
    local_blocks = panel_rows.shape[0] // block_size
    per_owner = max(2, 2 * slot_count // device_count)
    buffer_slots = device_count * per_owner
    targets = block_owner[:, 0]
    hits_table = (targets[:, None] == jnp.arange(device_count, dtype=jnp.int32)[None, :]).astype(
        jnp.int32
    )
    earlier = jnp.cumsum(hits_table, axis=0) - hits_table
    order_in = jnp.sum(earlier * hits_table, axis=1)
    position = targets * per_owner + order_in
    labels = (
        jnp.full((buffer_slots,), -1.0, jnp.float32)
        .at[position]
        .set(block_offset.astype(jnp.float32))
    )
    labels = labels.reshape(row_count, col_count, per_owner)
    panel_blocks = panel_rows.reshape(local_blocks, block_size, width)[block_row]
    local_products = jnp.einsum(
        "sij,sik->sjk", sparse_blocks, panel_blocks, precision=lax.Precision.HIGHEST
    )
    send_products = (
        jnp.zeros((buffer_slots, block_size, width), jnp.float32).at[position].set(local_products)
    )
    send_products = send_products.reshape(row_count, col_count, per_owner, block_size, width)
    arrived, arrived_labels = relay_single(send_products, labels)
    products = arrived.reshape(buffer_slots, block_size * width)
    flat_labels = arrived_labels.reshape(buffer_slots)
    onehot = (flat_labels[None, :] == jnp.arange(local_blocks, dtype=jnp.float32)[:, None]).astype(
        jnp.float32
    )
    summed = jnp.dot(
        onehot, products, precision=lax.Precision.HIGHEST, preferred_element_type=jnp.float32
    )
    return summed.reshape(local_blocks * block_size, width)


def solution(mesh):
    placed = (
        P(("row", "col"), None, None),
        P(("row", "col"), None),
        P(("row", "col")),
        P(("row", "col"), None),
        P(("row", "col")),
    )
    return jax.shard_map(
        body, mesh=mesh, in_specs=placed, out_specs=P(("row", "col"), None), check_vma=False
    )
```

profile of v0, /device:TPU:6, one launch (start us, length us, event | category | flops | bytes accessed | tf_op | source)
XLA Modules:
  0.0 482.8 jit_solution(11468233127488391712)
XLA Ops:
  0.0 0.7 fusion.3
  0.7 0.2 reduce_window_sum.11
  0.9 0.8 select_reduce_fusion
  1.7 0.7 fusion.5
  2.4 0.7 convert_element_type.8
  3.1 1.0 scatter_custom_fusion
  4.1 0.7 all_to_all.9
  4.8 6.1 %all-to-all-start = ((f32[32,1,8]{2,1,0:T(1,128)}), f32[32,1,8]{2,1,0:T(1,128)S(1)}, u32[]{:S(2)}, u32[]{:S(2)}) async-start(f32[32,1,8]{2,1,0:T(1,128)} %bitcast.3), calls=%async_computation | async-start | bytes 32768 | tf_op jit(solution)/shard_map/all_to_all | solution.py:16
  10.8 0.7 compare_select_fusion
  11.5 6.5 %gather_fusion = f32[128,128,128]{2,1,0:T(8,128)} fusion(f32[64,128,128]{2,1,0:T(8,128)} %bitcast.20, s32[1024]{0:T(1024)S(1)} %pad_clamp_fusion), kind=kCustom, calls=%fused_computation | custom fusion | bytes 16777728 | tf_op jit(solution)/shard_map/gather | solution.py:43
  18.0 19.0 %convolution_bitcast_fusion = f32[128,128,128]{1,2,0:T(8,128)} fusion(f32[128,128,128]{2,1,0:T(8,128)} %gather_fusion, f32[128,128,128]{2,1,0:T(8,128)} %param.5), kind=kOutput, calls=%fused_computation.6 | convolution fusion | flops 3221225472 | bytes 25165824 | tf_op jit(solution)/shard_map/sij,sik->sjk/dot_general | solution.py:44
  37.0 9.0 %copy.11 = f32[128,128,128]{2,1,0:T(8,128)} copy(f32[128,128,128]{1,2,0:T(8,128)} %convolution_bitcast_fusion) | data formatting | bytes 16777216 | tf_op jit(solution)/shard_map/sij,sik->sjk/dot_general | solution.py:44
  46.0 7.8 %broadcast_in_dim.14 = f32[256,128,128]{2,1,0:T(8,128)} broadcast(f32[]{:T(128)} %constant.5.clone.1), dimensions={} | broadcast | bytes 16777220 | tf_op jit(solution)/shard_map/broadcast_in_dim | solution.py:48
  53.9 23.4 %scatter_fusion = f32[256,128,128]{2,1,0:T(8,128)} fusion(f32[256,128,128]{2,1,0:T(8,128)} %broadcast_in_dim.14, s32[128]{0:T(128)S(1)} %fusion.5, f32[128,128,128]{2,1,0:T(8,128)} %copy.11), kind=kCustom, calls=%fused_computation.2 | custom fusion | bytes 25166336 | tf_op jit(solution)/shard_map/scatter | solution.py:48
  77.3 0.0 all-to-all-done
  77.3 5.8 %all-to-all-start.1 = ((f32[32,8,128,128]{3,2,1,0:T(8,128)}), f32[32,8,128,128]{3,2,1,0:T(8,128)}, u32[]{:S(2)}, u32[]{:S(2)}) async-start(f32[32,8,128,128]{3,2,1,0:T(8,128)} %bitcast.19), calls=%async_computation.1 | async-start | bytes 33554432 | tf_op jit(solution)/shard_map/all_to_all | solution.py:13
  83.1 0.5 broadcast.29
  83.6 0.7 reduce.3
  84.3 0.1 eq.34
  84.4 377.7 %all-to-all-done.1 = f32[32,8,128,128]{3,2,1,0:T(8,128)} async-done(((f32[32,8,128,128]{3,2,1,0:T(8,128)}), f32[32,8,128,128]{3,2,1,0:T(8,128)}, u32[]{:S(2)}, u32[]{:S(2)}) %all-to-all-start.1) | async-done | bytes 16777248 | tf_op jit(solution)/shard_map/all_to_all | solution.py:13
  462.1 15.7 %fusion = f32[64,16384]{1,0:T(8,128)} fusion(f32[32,8,128,128]{3,2,1,0:T(8,128)} %all-to-all-done.1, f32[256]{0:T(256)S(1)} %eq.34), kind=kOutput, calls=%fused_computation.3 | convolution fusion | flops 3221241856 | bytes 20972544 | tf_op jit(solution)/shard_map/dot_general | solution.py:57
  477.9 4.9 %reshape.17 = f32[8192,128]{1,0:T(8,128)} reshape(f32[64,16384]{1,0:T(8,128)} %fusion) | data formatting | bytes 8388608 | tf_op jit(solution)/shard_map/reshape | solution.py:60
  (1 shorter events, 0.0 us)
Async XLA Ops:
  4.8 72.6 %all-to-all-start = ((f32[32,1,8]{2,1,0:T(1,128)}), f32[32,1,8]{2,1,0:T(1,128)S(1)}, u32[]{:S(2)}, u32[]{:S(2)}) async-start(f32[32,1,8]{2,1,0:T(1,128)} %bitcast.3), calls=%async_computation | async-start | bytes 32768 | tf_op jit(solution)/shard_map/all_to_all | solution.py:16
  77.3 384.8 %all-to-all-start.1 = ((f32[32,8,128,128]{3,2,1,0:T(8,128)}), f32[32,8,128,128]{3,2,1,0:T(8,128)}, u32[]{:S(2)}, u32[]{:S(2)}) async-start(f32[32,8,128,128]{3,2,1,0:T(8,128)} %bitcast.19), calls=%async_computation.1 | async-start | bytes 33554432 | tf_op jit(solution)/shard_map/all_to_all | solution.py:13
where the time goes:
time: 484 us; the launch traced here: 483 us
  waiting for transfers between devices  378 us (78%)
  local copies, waits for them, and re-layouts  53.9 us (11%)
  matrix products  34.7 us (7%)
  starting transfers between devices  11.9 us (2%)
    all_to_all x1, waiting for transfers between devices, relay_single(): lax.all_to_all(merge_lead(send_products), ('row', 'col'), split_axis=0, c...  378 us
    scatter x1, local copies, waits for them, and re-layouts, body(): jnp.zeros((buffer_slots, block_size, width), jnp.float32).at[position]  23.4 us
    dot_general x1, matrix products, body(): jnp.einsum('sij,sik->sjk', sparse_blocks, panel_blocks, precision=lax.Pre...  19 us
    dot_general x1, matrix products, body(): jnp.dot(onehot, products, precision=lax.Precision.HIGHEST, preferred_elem...  15.7 us
  transfers between devices with their start and end apart: 2, of which 1 were waited for; matrix products, arithmetic and copies ran while one was open for 14% of the time, Pallas kernels for 0%

commit v1 on v0

v1 whole, which is shorter than its diff:
```python
import functools

import jax
import jax.numpy as jnp
from jax import lax
from jax.experimental import pallas as pl
from jax.experimental.pallas import tpu as pltpu
from jax.sharding import PartitionSpec as P

AXES = ("row", "col")
VMEM_LIMIT = 60 * 1024 * 1024


def split_parts(value):
    high = value.astype(jnp.bfloat16)
    low = (value - high.astype(jnp.float32)).astype(jnp.bfloat16)
    return high, low


def block_product(block, panel):
    block_high, block_low = split_parts(block)
    panel_high, panel_low = split_parts(panel)
    dims = (((0,), (0,)), ((), ()))
    dot = functools.partial(lax.dot_general, dimension_numbers=dims, preferred_element_type=jnp.float32)
    return dot(
        jnp.concatenate([block_high, block_low], axis=0),
        jnp.concatenate([panel_high, panel_high], axis=0),
    ) + dot(block_high, panel_low)


def product_kernel(group, source_ref, row_ref, sparse_ref, panel_ref, out_ref):
    step = pl.program_id(0)
    for k in range(group):
        source = source_ref[step * group + k]

        @pl.when(source >= 0)
        def _():
            row = row_ref[jnp.maximum(source, 0)]
            out_ref[k] = block_product(sparse_ref[jnp.maximum(source, 0)], panel_ref[row])

        @pl.when(source < 0)
        def _():
            out_ref[k] = jnp.zeros(out_ref.shape[1:], jnp.float32)


def send_products(source, block_row, sparse_blocks, panel_blocks):
    slots = source.shape[0]
    count, size, _ = sparse_blocks.shape
    local_blocks, _, width = panel_blocks.shape
    group = min(8, slots)
    whole = lambda step, *_: (0, 0, 0)
    return pl.pallas_call(
        functools.partial(product_kernel, group),
        grid_spec=pltpu.PrefetchScalarGridSpec(
            num_scalar_prefetch=2,
            grid=(slots // group,),
            in_specs=[
                pl.BlockSpec((count, size, size), whole),
                pl.BlockSpec((local_blocks, size, width), whole),
            ],
            out_specs=pl.BlockSpec((group, size, width), lambda step, *_: (step, 0, 0)),
        ),
        out_shape=jax.ShapeDtypeStruct((slots, size, width), jnp.float32),
        compiler_params=pltpu.CompilerParams(vmem_limit_bytes=VMEM_LIMIT),
        cost_estimate=pl.CostEstimate(
            flops=6 * slots * size * size * width,
            bytes_accessed=4 * (count * size * size + (local_blocks + slots) * size * width),
            transcendentals=0,
        ),
    )(source, block_row, sparse_blocks, panel_blocks)


def collect_kernel(group, label_ref, arrived_ref, out_ref):
    step = pl.program_id(0)

    @pl.when(step == 0)
    def _():
        out_ref[...] = jnp.zeros(out_ref.shape, jnp.float32)

    for k in range(group):
        label = label_ref[step * group + k]

        @pl.when(label >= 0)
        def _():
            out_ref[jnp.maximum(label, 0)] += arrived_ref[k]


def collect(labels, arrived, local_blocks):
    slots, size, width = arrived.shape
    group = min(8, slots)
    return pl.pallas_call(
        functools.partial(collect_kernel, group),
        grid_spec=pltpu.PrefetchScalarGridSpec(
            num_scalar_prefetch=1,
            grid=(slots // group,),
            in_specs=[pl.BlockSpec((group, size, width), lambda step, *_: (step, 0, 0))],
            out_specs=pl.BlockSpec((local_blocks, size, width), lambda step, *_: (0, 0, 0)),
        ),
        out_shape=jax.ShapeDtypeStruct((local_blocks, size, width), jnp.float32),
        compiler_params=pltpu.CompilerParams(vmem_limit_bytes=VMEM_LIMIT),
        cost_estimate=pl.CostEstimate(
            flops=slots * size * width,
            bytes_accessed=4 * (slots + local_blocks) * size * width,
            transcendentals=0,
        ),
    )(labels, arrived)


def body(sparse_blocks, panel_rows, block_row, block_owner, block_offset):
    device_count = lax.axis_size("row") * lax.axis_size("col")
    half_count = device_count // 2
    slot_count, size, _ = sparse_blocks.shape
    width = panel_rows.shape[1]
    local_blocks = panel_rows.shape[0] // size
    per_owner = max(2, 2 * slot_count // device_count)
    half_slots = half_count * per_owner
    me = lax.axis_index(AXES)
    my_half = me // half_count
    groups = [list(range(half_count)), list(range(half_count, device_count))]
    exchange = functools.partial(
        lax.all_to_all, axis_name=AXES, split_axis=0, concat_axis=0, tiled=True, axis_index_groups=groups
    )

    owner = block_owner[:, 0]
    index = jnp.arange(slot_count, dtype=jnp.int32)
    earlier = (owner[:, None] == owner[None, :]) & (index[None, :] < index[:, None])
    order = jnp.sum(earlier.astype(jnp.int32), axis=1)
    half_of = (owner // half_count != my_half).astype(jnp.int32)
    position = half_of * half_slots + (owner % half_count) * per_owner + order
    hit = position[None, :] == jnp.arange(2 * half_slots, dtype=jnp.int32)[:, None]
    source = jnp.max(jnp.where(hit, index[None, :], -1), axis=1)
    label = jnp.max(jnp.where(hit, block_offset[None, :], -1), axis=1).astype(jnp.float32)
    near_source, far_source = source[:half_slots], source[half_slots:]
    label = label.reshape(2, half_count, per_owner).transpose(1, 0, 2).reshape(half_count, 2 * per_owner)
    labels = exchange(label).reshape(half_count, 2, per_owner).astype(jnp.int32)
    near_labels = labels[:, 0].reshape(half_slots)
    far_labels = labels[:, 1].reshape(half_slots)

    panel_blocks = panel_rows.reshape(local_blocks, size, width)
    far_products = send_products(far_source, block_row, sparse_blocks, panel_blocks)
    far_arrived = exchange(far_products)
    near_products = send_products(near_source, block_row, sparse_blocks, panel_blocks)
    far_sums = collect(far_labels, far_arrived, local_blocks)
    far_sums, near_products = lax.optimization_barrier((far_sums, near_products))
    across = [(d, (d + half_count) % device_count) for d in range(device_count)]
    crossed = lax.ppermute(far_sums, AXES, across)
    near_arrived = exchange(near_products)
    near_sums = collect(near_labels, near_arrived, local_blocks)
    return (near_sums + crossed).reshape(local_blocks * size, width)


def solution(mesh):
    placed = (
        P(AXES, None, None),
        P(AXES, None),
        P(AXES),
        P(AXES, None),
        P(AXES),
    )
    return jax.shard_map(
        body, mesh=mesh, in_specs=placed, out_specs=P(AXES, None), check_vma=False
    )
```

time: 484 us -> 410 us (0.85)
  waiting for transfers between devices: 378 us -> 309 us
  Pallas kernels: 0 us -> 68.7 us
  local copies, waits for them, and re-layouts: 53.9 us -> 2.83 us
  matrix products: 34.7 us -> 0 us
  starting transfers between devices: 11.9 us -> 18.4 us
    pallas_call x0 -> x4, Pallas kernels: none -> 68.7 us  [the longest x2 44 us: send_products(): pl.pallas_call(functools.partial(product_kernel, group), grid_spec=pltpu....]
    all_to_all x2 -> x3, waiting for transfers between devices: 378 us -> 309 us  [the longest x1 209 us: body(): near_arrived = exchange(near_products)]
    dot_general x2 -> x0, matrix products: 34.7 us -> none  [the longest x1 19 us: body(): jnp.einsum('sij,sik->sjk', sparse_blocks, panel_blocks, precision=lax.Pre...]
    scatter x2 -> x0, local copies, waits for them, and re-layouts: 24.4 us -> none  [the longest x1 23.4 us: body(): jnp.zeros((buffer_slots, block_size, width), jnp.float32).at[position]]
    dot_general x1 -> x0, local copies, waits for them, and re-layouts: 9 us -> none  [body(): jnp.einsum('sij,sik->sjk', sparse_blocks, panel_blocks, precision=lax.Pre...]
    broadcast_in_dim x1 -> x0, local copies, waits for them, and re-layouts: 7.84 us -> none  [body(): jnp.zeros((buffer_slots, block_size, width), jnp.float32).at[position]]
    add x0 -> x2, other arithmetic: none -> 7.24 us  [the longest x1 6.57 us: body(): return (near_sums + crossed).reshape(local_blocks * size, width)]
    gather x1 -> x0, local copies, waits for them, and re-layouts: 6.49 us -> none  [body(): panel_rows.reshape(local_blocks, block_size, width)[block_row]]
  transfers between devices with their start and end apart: 2 -> 4, of which waited for: 1 -> 2; matrix products, arithmetic and copies ran while one was open for 14% -> 0% of each run, Pallas kernels for 0% -> 14%
where the time goes in v1:
time: 410 us; the launch traced here: 408 us
  waiting for transfers between devices  309 us (75%)
  Pallas kernels  68.7 us (17%)
  starting transfers between devices  18.4 us (4%)
  other arithmetic  8.95 us (2%)
    all_to_all x1, waiting for transfers between devices, body(): near_arrived = exchange(near_products)  209 us
    all_to_all x1, waiting for transfers between devices, body(): far_arrived = exchange(far_products)  100 us
    pallas_call x2, Pallas kernels, send_products(): pl.pallas_call(functools.partial(product_kernel, group), grid_spec=pltpu....  44 us
    pallas_call x2, Pallas kernels, collect(): pl.pallas_call(functools.partial(collect_kernel, group), grid_spec=pltpu....  24.7 us
  transfers between devices with their start and end apart: 4, of which 2 were waited for; matrix products, arithmetic and copies ran while one was open for 0% of the time, Pallas kernels for 14%

profile of v1, /device:TPU:6, one launch (start us, length us, event | category | flops | bytes accessed | tf_op | source)
XLA Modules:
  0.0 408.0 jit_solution(18026039153996056351)
XLA Ops:
  0.0 0.9 convert_reduce_fusion
  0.9 0.7 fusion.2
  1.6 0.8 select_reduce_fusion
  2.4 0.1 convert_element_type.19
  2.5 0.1 copy.14
  2.6 0.7 copy.15
  3.2 5.2 %all-to-all-start = ((f32[16,1,16]{2,1,0:T(1,128)}), f32[16,1,16]{2,1,0:T(1,128)S(1)}, u32[]{:S(2)}, u32[]{:S(2)}) async-start(f32[16,1,16]{2,1,0:T(1,128)} %copy.15), calls=%async_computation | async-start | bytes 16384 | tf_op jit(solution)/shard_map/all_to_all | solution.py:135
  8.5 0.5 fusion.5
  9.0 21.5 %shard_map.55 = f32[128,128,128]{2,1,0:T(8,128)} custom-call(s32[128]{0:T(128)} %get-tuple-element.14.source_ref, s32[128]{0:T(128)} %row_ref.3, f32[128,128,128]{2,1,0:T(8,128)} %sparse_ref.3, f32[64,128,128]{2,1,0:T(8,128)} %bitcast.12), custom_call_target="tpu_custom_call" | custom-call | flops 1610612736 | bytes 20971520 | tf_op jit(solution)/shard_map/pallas_call | solution.py:52
  30.6 0.0 all-to-all-done
  30.6 5.6 %all-to-all-start.1 = ((f32[128,128,128]{2,1,0:T(8,128)}), f32[128,128,128]{2,1,0:T(8,128)}, u32[]{:S(2)}, u32[]{:S(2)}) async-start(f32[128,128,128]{2,1,0:T(8,128)} %shard_map.55), calls=%async_computation.1 | async-start | bytes 16777216 | tf_op jit(solution)/shard_map/all_to_all | solution.py:141
  36.1 22.4 %shard_map.57 = f32[128,128,128]{2,1,0:T(8,128)} custom-call(s32[128]{0:T(128)} %get-tuple-element.13.source_ref, s32[128]{0:T(128)} %row_ref.3, f32[128,128,128]{2,1,0:T(8,128)} %sparse_ref.3, f32[64,128,128]{2,1,0:T(8,128)} %bitcast.13), custom_call_target="tpu_custom_call" | custom-call | flops 1610612736 | bytes 20971520 | tf_op jit(solution)/shard_map/pallas_call | solution.py:52
  58.5 0.1 copy.16
  58.6 0.1 copy.18
  58.7 0.6 reshape_squeeze.7.label_ref
  59.3 100.0 %all-to-all-done.1.arrived_ref = f32[128,128,128]{2,1,0:T(8,128)} async-done(((f32[128,128,128]{2,1,0:T(8,128)}), f32[128,128,128]{2,1,0:T(8,128)}, u32[]{:S(2)}, u32[]{:S(2)}) %all-to-all-start.1) | async-done | bytes 8388640 | tf_op jit(solution)/shard_map/all_to_all | solution.py:141
  159.3 12.3 %shard_map.56 = f32[64,128,128]{2,1,0:T(8,128)} custom-call(s32[128]{0:T(128)} %reshape_squeeze.7.label_ref, f32[128,128,128]{2,1,0:T(8,128)} %all-to-all-done.1.arrived_ref), custom_call_target="tpu_custom_call" | custom-call | flops 2097152 | bytes 12582912 | tf_op jit(solution)/shard_map/pallas_call | solution.py:91
  171.6 4.6 %all-to-all-start.2 = ((f32[128,128,128]{2,1,0:T(8,128)}), f32[128,128,128]{2,1,0:T(8,128)}, u32[]{:S(2)}, u32[]{:S(2)}) async-start(f32[128,128,128]{2,1,0:T(8,128)} %shard_map.57), calls=%async_computation.2 | async-start | bytes 16777216 | tf_op jit(solution)/shard_map/all_to_all | solution.py:147
  176.2 3.0 collective-permute-start
  179.3 0.1 copy.17
  179.3 0.6 reshape_squeeze.6.label_ref
  180.0 209.1 %all-to-all-done.2.arrived_ref = f32[128,128,128]{2,1,0:T(8,128)} async-done(((f32[128,128,128]{2,1,0:T(8,128)}), f32[128,128,128]{2,1,0:T(8,128)}, u32[]{:S(2)}, u32[]{:S(2)}) %all-to-all-start.2) | async-done | bytes 8388640 | tf_op jit(solution)/shard_map/all_to_all | solution.py:147
  389.1 12.4 %shard_map.58 = f32[64,128,128]{2,1,0:T(8,128)} custom-call(s32[128]{0:T(128)} %reshape_squeeze.6.label_ref, f32[128,128,128]{2,1,0:T(8,128)} %all-to-all-done.2.arrived_ref), custom_call_target="tpu_custom_call" | custom-call | flops 2097152 | bytes 12582912 | tf_op jit(solution)/shard_map/pallas_call | solution.py:91
  401.5 0.0 collective-permute-done
  401.5 6.6 %add.40 = f32[64,128,128]{2,1,0:T(8,128)} add(f32[64,128,128]{2,1,0:T(8,128)} %shard_map.58, f32[64,128,128]{2,1,0:T(8,128)} %collective-permute-done) | non-fusion elementwise | flops 1048576 | bytes 12582912 | tf_op jit(solution)/shard_map/add | solution.py:149
  (3 shorter events, 0.0 us)
Async XLA Ops:
  3.2 27.3 %all-to-all-start = ((f32[16,1,16]{2,1,0:T(1,128)}), f32[16,1,16]{2,1,0:T(1,128)S(1)}, u32[]{:S(2)}, u32[]{:S(2)}) async-start(f32[16,1,16]{2,1,0:T(1,128)} %copy.15), calls=%async_computation | async-start | bytes 16384 | tf_op jit(solution)/shard_map/all_to_all | solution.py:135
  30.6 128.7 %all-to-all-start.1 = ((f32[128,128,128]{2,1,0:T(8,128)}), f32[128,128,128]{2,1,0:T(8,128)}, u32[]{:S(2)}, u32[]{:S(2)}) async-start(f32[128,128,128]{2,1,0:T(8,128)} %shard_map.55), calls=%async_computation.1 | async-start | bytes 16777216 | tf_op jit(solution)/shard_map/all_to_all | solution.py:141
  171.6 217.5 %all-to-all-start.2 = ((f32[128,128,128]{2,1,0:T(8,128)}), f32[128,128,128]{2,1,0:T(8,128)}, u32[]{:S(2)}, u32[]{:S(2)}) async-start(f32[128,128,128]{2,1,0:T(8,128)} %shard_map.57), calls=%async_computation.2 | async-start | bytes 16777216 | tf_op jit(solution)/shard_map/all_to_all | solution.py:147
  176.2 225.2 %collective-permute-start = (f32[64,128,128]{2,1,0:T(8,128)}, f32[64,128,128]{2,1,0:T(8,128)}, u32[]{:S(2)}, u32[]{:S(2)}) collective-permute-start(f32[64,128,128]{2,1,0:T(8,128)} %shard_map.56), channel_id=1, source_target_pairs={{0,16},{1,17},{2,18},{3,19},{4,20},{5,21},{6,22},{7,23},{8,24},{9,... | collective-permute-start | bytes 12582920 | tf_op jit(solution)/shard_map/ppermute | solution.py:146
